TPU v7x, 16 devices: a 4x2x1 block of a 4x4x8 slice. The times are simulated.
16 devices in a mesh: dp: 2 (over y, z), sp: 8 (over x, core).
Axes of the slice: x: 4, y: 2, z: 1, core: 2. Of those that a mesh axis runs over, the one named last changes fastest.
The devices are a block of a 4x4x8 slice.
Arguments:
- x: bfloat16 [2048, 6144], P(('dp', 'sp')), parts along dimension 0
- wq: bfloat16 [6144, 6144], replicated
- wk: bfloat16 [6144, 1024], replicated
- wv: bfloat16 [6144, 1024], replicated
- wo: bfloat16 [6144, 6144], replicated
- idx: int32 [2048, 4], P(('dp', 'sp')), parts along dimension 0
- probs: float32 [2048, 16], P(('dp', 'sp')), parts along dimension 0
Outputs:
- output 1: bfloat16 [2048, 6144], P(('dp', 'sp')), parts along dimension 0
- output 2: bfloat16 [32, 512, 6144], P(('dp', 'sp')), parts along dimension 0
There are 2 independent parts. A program takes and returns all parts, laid end to end along the dimension named above; an argument that names none is the same for every part.
All inputs are finite; a program needn't handle non-finite values.
Results may differ from a plain program's by a relative error of at most 0.00215937.
Values are sent between devices in bfloat16 or wider.
A program may use at most 768 MiB of HBM per device.

v0:
```python
import math
import jax
import jax.numpy as jnp
from jax import lax
from jax.sharding import PartitionSpec as P

HEAD = 128
ROPE_BASE = 1000000.0


def rope(t, pos):
    half = t.shape[-1] // 2
    inv = ROPE_BASE ** (-jnp.arange(half, dtype=jnp.float32) * (2.0 / t.shape[-1]))
    ang = pos.astype(jnp.float32)[:, None] * inv[None, :]
    c = jnp.cos(ang)[:, None, :]
    s = jnp.sin(ang)[:, None, :]
    a = t[..., :half]
    b = t[..., half:]
    return jnp.concatenate([a * c - b * s, b * c + a * s], axis=-1)


def attend(q, kt, vt, qpos, last=None):
    sq_len, g, m, d = q.shape
    sk_len = kt.shape[1]
    lim = max(8, 2 ** int(math.log2(max(1, 2048 // (g * m)))))
    qb = math.gcd(sq_len, min(128, lim))
    nb = sq_len // qb
    scale = 1.0 / math.sqrt(d)
    qs = q.reshape(nb, qb, g, m, d).transpose(0, 2, 3, 1, 4)
    ps = qpos.reshape(nb, qb)
    kl = [sk_len] * nb
    if last is not None:
        gran = -(-sk_len // 8)
        kl = [min(sk_len, -(-(last(j * qb + qb - 1) + 1) // gran) * gran) for j in range(nb)]

    def run(qq, pp, n_k):
        kk = kt[:, :n_k]
        vv = vt[:, :n_k]
        kpos = jnp.arange(n_k)

        def block(a):
            qj, pj = a
            sc = jnp.einsum("gmqd,gkd->gmqk", qj, kk, preferred_element_type=jnp.float32) * scale
            keep = kpos[None, :] <= pj[:, None]
            sc = jnp.where(keep[None, None], sc, -jnp.inf)
            p = jax.nn.softmax(sc, axis=-1).astype(jnp.bfloat16)
            o = jnp.einsum("gmqk,gkd->gmqd", p, vv, preferred_element_type=jnp.float32)
            return o.astype(jnp.bfloat16)

        return lax.map(block, (qq, pp))

    outs = []
    j = 0
    while j < nb:
        e = j
        while e < nb and kl[e] == kl[j]:
            e += 1
        outs.append(run(qs[j:e], ps[j:e], kl[j]))
        j = e
    o = outs[0] if len(outs) == 1 else jnp.concatenate(outs, axis=0)
    return o.transpose(0, 3, 1, 2, 4).reshape(sq_len, g, m, d)


def route(idx, probs, cap):
    sd = idx.shape[0]
    ne = probs.shape[1]
    hot = idx[:, :, None] == jnp.arange(ne)[None, None, :]
    sel = jnp.sum(jnp.where(hot, probs[:, None, :], 0.0), axis=2)
    w = sel / jnp.sum(sel, axis=1, keepdims=True)
    gate = jnp.sum(jnp.where(hot, w[:, :, None], 0.0), axis=1)
    mine = jnp.any(hot, axis=1)
    tok = jnp.arange(sd)
    low = (tok[None, :] < tok[:, None]).astype(jnp.bfloat16)
    rank = jnp.dot(low, mine.astype(jnp.bfloat16), preferred_element_type=jnp.float32).astype(jnp.int32)
    pick = (rank.T[:, None, :] == jnp.arange(cap)[None, :, None]) & mine.T[:, None, :]
    ws = jnp.sum(jnp.where(pick, gate.T[:, None, :], 0.0), axis=2)
    return pick.astype(jnp.bfloat16), ws


def spread(h, pick, ws):
    hg = jnp.einsum("ect,th->ech", pick, h, preferred_element_type=jnp.bfloat16)
    return (ws[:, :, None] * hg.astype(jnp.float32)).astype(jnp.bfloat16)


def dispatch_rows(h, idx, probs, cap):
    pick, ws = route(idx, probs, cap)
    return spread(h, pick, ws)


def solution(mesh):
    n = mesh.shape["sp"]
    row = P(("dp", "sp"), None)
    full = P(None, None)

    def local(x, wq, wk, wv, wo, idx, probs):
        sd, hid = x.shape
        heads = wq.shape[1] // HEAD
        kvh = wk.shape[1] // HEAD
        m = heads // kvh
        ne = probs.shape[1]
        cap = 2 * sd * idx.shape[1] // ne
        me = lax.axis_index("sp")
        pos = me * sd + jnp.arange(sd)
        q = rope(jnp.dot(x, wq, preferred_element_type=jnp.float32).reshape(sd, heads, HEAD), pos)
        k = rope(jnp.dot(x, wk, preferred_element_type=jnp.float32).reshape(sd, kvh, HEAD), pos)
        q = q.astype(jnp.bfloat16).reshape(sd, heads * HEAD)
        k = k.astype(jnp.bfloat16).reshape(sd, kvh * HEAD)
        v = jnp.dot(x, wv, preferred_element_type=jnp.float32).astype(jnp.bfloat16)
        q = lax.all_to_all(q, "sp", 1, 0, tiled=True)
        k = lax.all_to_all(k, "sp", 1, 0, tiled=True)
        v = lax.all_to_all(v, "sp", 1, 0, tiled=True)
        s_len = n * sd
        g = kvh // n
        kt = k.reshape(s_len, g, HEAD).transpose(1, 0, 2)
        vt = v.reshape(s_len, g, HEAD).transpose(1, 0, 2)
        o = attend(q.reshape(s_len, g, m, HEAD), kt, vt, jnp.arange(s_len), lambda r: r)
        o = lax.all_to_all(o.reshape(s_len, g * m * HEAD), "sp", 0, 1, tiled=True)
        h = (x.astype(jnp.float32) + jnp.dot(o, wo, preferred_element_type=jnp.float32)).astype(jnp.bfloat16)
        send = dispatch_rows(h, idx, probs, cap)
        recv = lax.all_to_all(send, "sp", 0, 0, tiled=True)
        buf = recv.reshape(n, ne // n, cap, hid).transpose(1, 0, 2, 3).reshape(ne // n, n * cap, hid)
        return h, buf

    return jax.shard_map(local, mesh=mesh, in_specs=(row, full, full, full, full, row, row), out_specs=(row, P(("dp", "sp"), None, None)), check_vma=False)
```

profile of v0, /device:TPU:113, one launch (start us, length us, event | category | flops | bytes accessed | tf_op | source)
XLA Modules:
  0.0 333.9 jit_solution(9339466960481439310)
XLA Ops:
  0.7 28.4 %convolution_bitcast_fusion = f32[16,8,48,128]{3,1,2,0:T(8,128)} fusion(bf16[128,6144]{1,0:T(8,128)(2,1)} %param.7, bf16[6144,6144]{1,0:T(8,128)(2,1)} %param.8), kind=kOutput, calls=%fused_computation.28 | convolution fusion | flops 9663676416 | bytes 80216064 | tf_op jit(solution)/shard_map/dot_general | solution.py:104
  29.0 2.4 copy.60
  33.9 1.8 copy.38
  35.7 6.1 %all-to-all-start = ((bf16[128,8,768]{0,2,1:T(8,128)(2,1)}), bf16[128,8,768]{0,2,1:T(8,128)(2,1)S(1)}, u32[]{:S(2)}, u32[]{:S(2)}) async-start(bf16[128,8,768]{0,2,1:T(8,128)(2,1)} %bitcast.320), calls=%async_computation | async-start | bytes 3145728 | tf_op jit(solution)/shard_map/all_to_all | solution.py:109
  44.7 6.8 %convolution_bitcast_fusion.1 = f32[16,8,8,128]{3,1,2,0:T(8,128)S(1)} fusion(bf16[128,6144]{1,0:T(8,128)(2,1)S(1)} %copy-done, bf16[6144,1024]{1,0:T(8,128)(2,1)} %param.9), kind=kOutput, calls=%fused_computation.53 | convolution fusion | flops 1610612736 | bytes 14680064 | tf_op jit(solution)/shard_map/dot_general | solution.py:105
  53.8 1.8 fusion.40
  55.6 6.6 %all-to-all-done = bf16[128,8,768]{0,2,1:T(8,128)(2,1)S(1)} async-done(((bf16[128,8,768]{0,2,1:T(8,128)(2,1)}), bf16[128,8,768]{0,2,1:T(8,128)(2,1)S(1)}, u32[]{:S(2)}, u32[]{:S(2)}) %all-to-all-start) | async-done | bytes 1572896 | tf_op jit(solution)/shard_map/all_to_all | solution.py:109
  62.2 5.1 %all-to-all-start.1 = ((bf16[128,8,128]{2,0,1:T(8,128)(2,1)}), bf16[128,8,128]{2,0,1:T(8,128)(2,1)}, u32[]{:S(2)}, u32[]{:S(2)}) async-start(bf16[128,8,128]{2,0,1:T(8,128)(2,1)} %pad_maximum_fusion.1), calls=%async_computation.1 | async-start | bytes 524288 | tf_op jit(solution)/shard_map/all_to_all | solution.py:110
  73.8 5.2 %all-to-all-start.2 = ((bf16[128,8,128]{2,0,1:T(8,128)(2,1)}), bf16[128,8,128]{2,0,1:T(8,128)(2,1)}, u32[]{:S(2)}, u32[]{:S(2)}) async-start(bf16[128,8,128]{2,0,1:T(8,128)(2,1)} %bitcast.313), calls=%async_computation.2 | async-start | bytes 524288 | tf_op jit(solution)/shard_map/all_to_all | solution.py:111
  79.0 2.0 fusion.121
  81.0 2.0 fusion.29
  83.0 2.1 fusion.122
  85.1 2.2 fusion.123
  87.3 2.7 fusion.126
  90.0 2.4 fusion.124
  93.4 1.6 fusion.120
  95.0 2.0 fusion.125
  97.1 1.7 fusion.52
  98.8 3.6 %fusion.44 = bf16[8,1,6,128,128]{3,4,2,1,0:T(8,128)(2,1)} fusion(bf16[8,1,6,128,128]{3,4,2,1,0:T(8,128)(2,1)} %fusion.52, f32[6,128]{1,0:T(8,128)S(1)} %copy-done.11, f32[6,128,256]{2,1,0:T(8,128)} %fusion.29, bf16[1,1024,128]{2,1,0:T(8,128)(2,1)} %bitcast.11), kind=kOutput, calls=%fused_computation.75 | convolution fusion | flops 51020800 | bytes 1838080 | tf_op jit(solution)/shard_map/while/body/eval_jaxpr/gmqk,gkd->gmqd/dot_general | solution.py:47
  102.3 3.3 fusion.46
  105.7 3.5 %fusion.42 = bf16[8,1,6,128,128]{3,4,2,1,0:T(8,128)(2,1)} fusion(bf16[8,1,6,128,128]{3,4,2,1,0:T(8,128)(2,1)} %fusion.46, f32[6,128]{1,0:T(8,128)S(1)} %copy-done.13, bf16[1,1024,128]{2,1,0:T(8,128)(2,1)} %bitcast.11, pred[128,512]{1,0:T(8,128)(4,1)} %iota_compare_fusion.5, bf16[8,1,6,128,128]{4,3,2,1,0:T(8,128)(2,1)S(1)} %bitcast.333, ...), kind=kOutput, calls=%fused_computation.73 | convolution fusion | flops 203392256 | bytes 724992 | tf_op jit(solution)/shard_map/while/body/eval_jaxpr/gmqk,gkd->gmqd/dot_general | solution.py:47
  109.2 3.8 %fusion.50 = bf16[8,1,6,128,128]{3,4,2,1,0:T(8,128)(2,1)} fusion(bf16[8,1,6,128,128]{3,4,2,1,0:T(8,128)(2,1)} %fusion.42, f32[6,128]{1,0:T(8,128)S(1)} %copy-done.14, bf16[1,1024,128]{2,1,0:T(8,128)(2,1)} %bitcast.11, pred[128,640]{1,0:T(8,128)(4,1)} %iota_compare_fusion.4, bf16[8,1,6,128,128]{4,3,2,1,0:T(8,128)(2,1)S(1)} %bitcast.334, ...), kind=kOutput, calls=%fused_computation.81 | convolution fusion | flops 254215552 | bytes 806912 | tf_op jit(solution)/shard_map/while/body/eval_jaxpr/gmqk,gkd->gmqd/dot_general | solution.py:47
  112.9 4.0 %fusion.54 = bf16[8,1,6,128,128]{3,4,2,1,0:T(8,128)(2,1)} fusion(bf16[8,1,6,128,128]{3,4,2,1,0:T(8,128)(2,1)} %fusion.50, f32[6,128]{1,0:T(8,128)S(1)} %fusion.125, bf16[1,1024,128]{2,1,0:T(8,128)(2,1)} %bitcast.11, pred[128,768]{1,0:T(8,128)(4,1)} %iota_compare_fusion.3, bf16[8,1,6,128,128]{4,3,2,1,0:T(8,128)(2,1)S(1)} %bitcast.335, ...), kind=kOutput, calls=%fused_computation.85 | convolution fusion | flops 305038848 | bytes 888832 | tf_op jit(solution)/shard_map/while/body/eval_jaxpr/gmqk,gkd->gmqd/dot_general | solution.py:47
  116.9 4.1 %fusion.48 = bf16[8,1,6,128,128]{3,4,2,1,0:T(8,128)(2,1)} fusion(bf16[8,1,6,128,128]{3,4,2,1,0:T(8,128)(2,1)} %fusion.54, f32[6,128]{1,0:T(8,128)S(1)} %copy-done.15, bf16[1,1024,128]{2,1,0:T(8,128)(2,1)} %bitcast.11, pred[128,896]{1,0:T(8,128)(4,1)} %copy-done.3, bf16[1,1024,128]{2,1,0:T(8,128)(2,1)} %bitcast.7, bf16[8,1,6,128,128]{4,3,2,1,0:T(8,128)(2,1)S(1)} %bitcast.336), kind=kOutput, calls=%fused_computation.79 | convolution fusion | flops 355862144 | bytes 970752 | tf_op jit(solution)/shard_map/while/body/eval_jaxpr/gmqk,gkd->gmqd/dot_general | solution.py:47
  121.1 3.8 %fusion.127 = (f32[6,128]{1,0:T(8,128)S(1)}, f32[6,128,1024]{2,1,0:T(8,128)}) fusion(pred[128,1024]{1,0:T(8,128)(4,1)S(1)} %copy-done.2, bf16[1024,128,1]{1,0,2:T(8,128)(2,1)} %bitcast.62, bf16[8,1,6,128,128]{4,3,2,1,0:T(8,128)(2,1)S(1)} %bitcast.337), kind=kOutput, calls=%fused_computation.201 | convolution fusion | flops 204473344 | bytes 3738624 | tf_op jit(solution)/shard_map/while/body/eval_jaxpr/sub | solution.py:46
  124.8 3.3 fusion.56
  128.2 5.0 %all-to-all-start.3 = ((bf16[8,128,768]{1,2,0:T(8,128)(2,1)}), bf16[8,128,768]{1,2,0:T(8,128)(2,1)S(1)}, u32[]{:S(2)}, u32[]{:S(2)}) async-start(bf16[8,128,768]{1,2,0:T(8,128)(2,1)} %bitcast.338), calls=%async_computation.3 | async-start | bytes 3145728 | tf_op jit(solution)/shard_map/all_to_all | solution.py:117
  133.6 19.9 %all-to-all-done.3 = bf16[8,128,768]{1,2,0:T(8,128)(2,1)S(1)} async-done(((bf16[8,128,768]{1,2,0:T(8,128)(2,1)}), bf16[8,128,768]{1,2,0:T(8,128)(2,1)S(1)}, u32[]{:S(2)}, u32[]{:S(2)}) %all-to-all-start.3) | async-done | bytes 1572896 | tf_op jit(solution)/shard_map/all_to_all | solution.py:117
  153.5 27.8 %fusion.8 = bf16[128,6144]{1,0:T(8,128)(2,1)} fusion(bf16[128,6144]{0,1:T(8,128)(2,1)S(1)} %bitcast.321, bf16[6144,6144]{1,0:T(8,128)(2,1)} %param.11, bf16[128,6144]{1,0:T(8,128)(2,1)S(1)} %copy-done), kind=kOutput, calls=%fused_computation.10 | convolution fusion | flops 9666035712 | bytes 80216064 | tf_op jit(solution)/shard_map/dot_general | solution.py:118
  181.3 5.0 %multiply_convert_fusion = bf16[16,64,6144]{2,1,0:T(8,128)(2,1)S(1)} fusion(f32[16,64]{1,0:T(8,128)S(1)} %select_reduce_fusion, bf16[128,6144]{1,0:T(8,128)(2,1)} %fusion.8, s32[16,128]{1,0:T(8,128)S(1)} %convolution_convert_fusion.6, pred[16,128]{1,0:T(8,128)(4,1)S(1)} %bitcast.340), kind=kOutput, calls=%fused_computation.8 | convolution fusion | flops 1629749248 | bytes 14170112 | tf_op jit(solution)/shard_map/ect,th->ech/dot_general | solution.py:81
  186.3 142.5 %all_to_all.66 = bf16[16,64,6144]{2,1,0:T(8,128)(2,1)S(1)} all-to-all(bf16[16,64,6144]{2,1,0:T(8,128)(2,1)S(1)} %multiply_convert_fusion), channel_id=1, replica_groups=mesh['dp'=2,'sp'=8] {'sp'}, dimensions={0} | all-to-all | bytes 25165824 | tf_op jit(solution)/shard_map/all_to_all | solution.py:120
  328.8 5.1 %copy.46 = bf16[2,8,64,6144]{3,2,1,0:T(8,128)(2,1)} copy(bf16[2,8,64,6144]{3,2,0,1:T(8,128)(2,1)S(1)} %bitcast.314) | data formatting | bytes 25165824 | tf_op jit(solution)/shard_map/transpose | solution.py:121
  (69 shorter events, 15.4 us)
Async XLA Ops:
  35.7 9.0 %copy-start = (bf16[128,6144]{1,0:T(8,128)(2,1)S(1)}, bf16[128,6144]{1,0:T(8,128)(2,1)}, u32[]{:S(2)}) copy-start(bf16[128,6144]{1,0:T(8,128)(2,1)} %param.7) | copy-start | bytes 4718596
  35.7 26.5 %all-to-all-start = ((bf16[128,8,768]{0,2,1:T(8,128)(2,1)}), bf16[128,8,768]{0,2,1:T(8,128)(2,1)S(1)}, u32[]{:S(2)}, u32[]{:S(2)}) async-start(bf16[128,8,768]{0,2,1:T(8,128)(2,1)} %bitcast.320), calls=%async_computation | async-start | bytes 3145728 | tf_op jit(solution)/shard_map/all_to_all | solution.py:109
  44.0 9.8 %slice-start = ((s8[12582912]{0:T(1024)(128)(4,1)}), s8[4194304]{0:T(1024)(128)(4,1)S(1)}, s32[]{:S(2)}) async-start(s8[12582912]{0:T(1024)(128)(4,1)} %bitcast.316), calls=%async_computation.5 | async-start | bytes 8388608
  44.7 9.1 %slice-start.1 = ((s8[12582912]{0:T(1024)(128)(4,1)}), s8[4194304]{0:T(1024)(128)(4,1)S(1)}, s32[]{:S(2)}) async-start(s8[12582912]{0:T(1024)(128)(4,1)} %bitcast.316), calls=%async_computation.6 | async-start | bytes 8388608
  44.7 9.1 %slice-start.2 = ((s8[12582912]{0:T(1024)(128)(4,1)}), s8[4194304]{0:T(1024)(128)(4,1)S(1)}, s32[]{:S(2)}) async-start(s8[12582912]{0:T(1024)(128)(4,1)} %bitcast.316), calls=%async_computation.7 | async-start | bytes 8388608
  53.8 33.4 %copy-start.3 = (pred[128,896]{1,0:T(8,128)(4,1)}, pred[128,896]{1,0:T(8,128)(4,1)S(1)}, u32[]{:S(2)}) copy-start(pred[128,896]{1,0:T(8,128)(4,1)S(1)} %iota_compare_fusion.2) | copy-start | bytes 344068
  62.2 11.5 %all-to-all-start.1 = ((bf16[128,8,128]{2,0,1:T(8,128)(2,1)}), bf16[128,8,128]{2,0,1:T(8,128)(2,1)}, u32[]{:S(2)}, u32[]{:S(2)}) async-start(bf16[128,8,128]{2,0,1:T(8,128)(2,1)} %pad_maximum_fusion.1), calls=%async_computation.1 | async-start | bytes 524288 | tf_op jit(solution)/shard_map/all_to_all | solution.py:110
  72.4 8.6 %copy-start.1 = (bf16[8,128,1,6,128]{4,1,3,2,0:T(8,128)(2,1)S(1)}, bf16[8,128,1,6,128]{4,1,3,2,0:T(8,128)(2,1)}, u32[]{:S(2)}) copy-start(bf16[8,128,1,6,128]{4,1,3,2,0:T(8,128)(2,1)} %copy.39) | copy-start | bytes 4718596
  73.8 9.2 %copy-start.7 = (pred[128,384]{1,0:T(8,128)(4,1)S(1)}, pred[128,384]{1,0:T(8,128)(4,1)}, u32[]{:S(2)}) copy-start(pred[128,384]{1,0:T(8,128)(4,1)} %iota_compare_fusion.6) | copy-start | bytes 147460
  73.8 23.3 %all-to-all-start.2 = ((bf16[128,8,128]{2,0,1:T(8,128)(2,1)}), bf16[128,8,128]{2,0,1:T(8,128)(2,1)}, u32[]{:S(2)}, u32[]{:S(2)}) async-start(bf16[128,8,128]{2,0,1:T(8,128)(2,1)} %bitcast.313), calls=%async_computation.2 | async-start | bytes 524288 | tf_op jit(solution)/shard_map/all_to_all | solution.py:111
  81.0 4.1 %copy-start.6 = (pred[128,512]{1,0:T(8,128)(4,1)S(1)}, pred[128,512]{1,0:T(8,128)(4,1)}, u32[]{:S(2)}) copy-start(pred[128,512]{1,0:T(8,128)(4,1)} %iota_compare_fusion.5) | copy-start | bytes 196612
  87.3 2.7 copy-start.4
  90.0 2.4 copy-start.5
  95.0 2.0 copy-start.10
  97.0 1.7 copy-start.11
  98.8 3.6 %copy-start.12 = (f32[6,128]{1,0:T(8,128)S(1)}, f32[6,128]{1,0:T(8,128)}, u32[]{:S(2)}) copy-start(f32[6,128]{1,0:T(8,128)} %fusion.122) | copy-start | bytes 9220
  102.3 3.3 copy-start.13
  105.7 3.5 %copy-start.14 = (f32[6,128]{1,0:T(8,128)S(1)}, f32[6,128]{1,0:T(8,128)}, u32[]{:S(2)}) copy-start(f32[6,128]{1,0:T(8,128)} %fusion.124) | copy-start | bytes 9220
  112.9 4.0 %copy-start.15 = (f32[6,128]{1,0:T(8,128)S(1)}, f32[6,128]{1,0:T(8,128)}, u32[]{:S(2)}) copy-start(f32[6,128]{1,0:T(8,128)} %fusion.126) | copy-start | bytes 9220
  116.9 4.1 %copy-start.2 = (pred[128,1024]{1,0:T(8,128)(4,1)S(1)}, pred[128,1024]{1,0:T(8,128)(4,1)}, u32[]{:S(2)}) copy-start(pred[128,1024]{1,0:T(8,128)(4,1)} %iota_compare_fusion.1) | copy-start | bytes 393220
  128.2 5.0 %copy-start.8 = (s32[128,4]{0,1:T(4,128)S(1)}, s32[128,4]{0,1:T(4,128)}, u32[]{:S(2)}) copy-start(s32[128,4]{0,1:T(4,128)} %param.12) | copy-start | bytes 6148
  128.2 5.0 %copy-start.9 = (f32[128,16]{0,1:T(8,128)S(1)}, f32[128,16]{0,1:T(8,128)}, u32[]{:S(2)}) copy-start(f32[128,16]{0,1:T(8,128)} %param.13) | copy-start | bytes 24580
  128.2 25.4 %all-to-all-start.3 = ((bf16[8,128,768]{1,2,0:T(8,128)(2,1)}), bf16[8,128,768]{1,2,0:T(8,128)(2,1)S(1)}, u32[]{:S(2)}, u32[]{:S(2)}) async-start(bf16[8,128,768]{1,2,0:T(8,128)(2,1)} %bitcast.338), calls=%async_computation.3 | async-start | bytes 3145728 | tf_op jit(solution)/shard_map/all_to_all | solution.py:117
where the time goes:
time: 335 us; the launch traced here: 334 us
  blocking collectives  143 us (43%)
  matrix products  119 us (36%)
  waiting for transfers between devices  27.9 us (8%)
  starting transfers between devices  21.5 us (6%)
  local copies, waits for them, and re-layouts  12.6 us (4%)
  other arithmetic  9.62 us (3%)
    all_to_all x1, blocking collectives, local(): recv = lax.all_to_all(send, 'sp', 0, 0, tiled=True)  143 us
    dot_general x1, matrix products, local(): jnp.dot(x, wq, preferred_element_type=jnp.float32).reshape(sd, heads, HEAD)  28.4 us
    dot_general x1, matrix products, local(): jnp.dot(o, wo, preferred_element_type=jnp.float32)  27.8 us
    dot_general x8, matrix products, block(): o = jnp.einsum('gmqk,gkd->gmqd', p, vv, preferred_element_type=jnp.float32)  27.3 us
    all_to_all x1, waiting for transfers between devices, local(): o = lax.all_to_all(o.reshape(s_len, g * m * HEAD), 'sp', 0, 1, tiled=True)  19.9 us
    sub x8, matrix products, block(): p = jax.nn.softmax(sc, axis=-1).astype(jnp.bfloat16)  18.8 us
    dot_general x1, matrix products, local(): jnp.dot(x, wk, preferred_element_type=jnp.float32).reshape(sd, kvh, HEAD)  6.76 us
  transfers between devices with their start and end apart: 4, of which 3 were waited for; matrix products, arithmetic and copies ran while one was open for 11% of the time, Pallas kernels for 0%

commit v1 on v0

v1 whole, which is shorter than its diff:
```python
import functools
import math
import numpy as np
import jax
import jax.numpy as jnp
from jax import lax
from jax.experimental import pallas as pl
from jax.experimental.pallas import tpu as pltpu
from jax.sharding import PartitionSpec as P

HEAD = 128
ROPE_BASE = 1000000.0
CORES = 2
COL = 256
F32 = jnp.float32
BF16 = jnp.bfloat16
MESH = pl.DeviceIdType.MESH


def rope_table(length):
    inv = ROPE_BASE ** (-np.arange(HEAD // 2, dtype=np.float64) * (2.0 / HEAD))
    ang = np.arange(length, dtype=np.float64)[:, None] * inv[None, :]
    c, s = np.cos(ang), np.sin(ang)
    return np.stack([np.concatenate([c, c], 1), np.concatenate([-s, s], 1)]).astype(np.float32)


def block_kernel(n, kvh, m, nb, x_ref, wq_ref, wk_ref, wv_ref, wo_ref, idx_ref, probs_ref, rope_ref,
                 hg_ref, tw_ref,
                 xf, wbuf, cs, kvb, qt, of, ho, st, tw_own,
                 w_sem, x_sem, tws_sem, twr_sem, kvs_sem, kvf_sem, kvr_sem, os_sem, or_sem,
                 hl_sem, hs_sem, hf_sem, hp_sem, hr_sem, pr_sem):
    sd, hid = x_ref.shape
    chips = n // CORES
    ct = CORES * sd
    heads_c = kvh // CORES
    nk = heads_c * HEAD // COL
    nq = heads_c * m * HEAD // COL
    no = hid // CORES // COL
    hpc = COL // HEAD
    me = lax.axis_index("sp")
    chip = lax.div(me, CORES)
    core = lax.rem(me, CORES)
    partner = me + 1 - 2 * core
    right = lax.rem(me + CORES, n)
    left = lax.rem(me + n - CORES, n)
    rchip = lax.rem(chip + 1, chips)
    lchip = lax.rem(chip + chips - 1, chips)
    fchip = lax.rem(chip + 2, chips)

    def ds(i, size):
        return pl.ds(pl.multiple_of(i, size), size)

    def wcopy(src, col0, slot):
        return pltpu.make_async_copy(src.at[:, ds(col0, COL)], wbuf.at[slot], w_sem.at[slot])

    def k_copy(i, slot):
        return wcopy(wk_ref, core * (heads_c * HEAD) + i * COL, slot)

    def v_copy(i, slot):
        return wcopy(wv_ref, core * (heads_c * HEAD) + i * COL, slot)

    def q_copy(i, slot):
        return wcopy(wq_ref, core * (nq * COL) + i * COL, slot)

    def o_copy(i, slot):
        return wcopy(wo_ref, core * (no * COL) + i * COL, slot)

    base_q = 2 * nk
    for i in range(nk):
        k_copy(i, 2 * i).start()
        v_copy(i, 2 * i + 1).start()
    own_x = pltpu.make_async_copy(x_ref, xf.at[ds(core * sd, sd)], x_sem.at[2])
    own_x.start()
    rope_cp = pltpu.make_async_copy(rope_ref.at[:, ds(chip * ct, ct)], cs, x_sem.at[3])
    rope_cp.start()
    for i in range(nb - base_q):
        q_copy(i, base_q + i).start()

    barrier = pltpu.get_barrier_semaphore()

    @pl.loop(1, n)
    def _(off):
        pl.semaphore_signal(barrier, inc=1, device_id={"sp": lax.rem(me + off, n)}, device_id_type=MESH)

    pl.semaphore_wait(barrier, n - 1)

    def remote(src, dst, ssem, rsem, dev):
        return pltpu.make_async_remote_copy(src_ref=src, dst_ref=dst, send_sem=ssem, recv_sem=rsem,
                                            device_id={"sp": dev}, device_id_type=MESH)

    x_send = remote(x_ref, xf.at[ds(core * sd, sd)], x_sem.at[0], x_sem.at[1], partner)
    x_send.start()

    ne = probs_ref.shape[1]
    top = idx_ref.shape[1]
    per = ne // n
    cap = 2 * sd * top // ne
    probs = probs_ref[...]
    ei = lax.broadcasted_iota(jnp.int32, (sd, ne), 1)
    mine = jnp.zeros((sd, ne), F32)
    tot = jnp.zeros((sd, 1), F32)
    for c in range(top):
        hot = idx_ref[:, c:c + 1] == ei
        mine = jnp.where(hot, 1.0, mine)
        sel = jnp.sum(jnp.where(hot, probs, 0.0), axis=1, keepdims=True)
        tot = sel if c == 0 else tot + sel
    gate = probs / tot
    low = (lax.broadcasted_iota(jnp.int32, (sd, sd), 1) < lax.broadcasted_iota(jnp.int32, (sd, sd), 0))
    rank = jnp.dot(jnp.where(low, 1.0, 0.0).astype(BF16), mine.astype(BF16), preferred_element_type=F32)
    rank = jnp.where(mine > 0.5, rank, -1.0)
    rows = per * cap
    lane = lax.broadcasted_iota(jnp.int32, (sd, rows), 1)
    tok1 = (lax.broadcasted_iota(jnp.int32, (sd, rows), 0) + 1).astype(F32)
    sub = lax.broadcasted_iota(jnp.int32, (8, rows), 0)
    for d in range(n):
        rk = jnp.broadcast_to(rank[:, per * d:per * d + 1], (sd, rows))
        gt = jnp.broadcast_to(gate[:, per * d:per * d + 1], (sd, rows))
        for k in range(1, per):
            rk = jnp.where(lane >= k * cap, rank[:, per * d + k:per * d + k + 1], rk)
            gt = jnp.where(lane >= k * cap, gate[:, per * d + k:per * d + k + 1], gt)
        hit = rk == lax.rem(lane, cap).astype(F32)
        t_row = jnp.sum(jnp.where(hit, tok1, 0.0), axis=0, keepdims=True) - 1.0
        w_row = jnp.sum(jnp.where(hit, gt, 0.0), axis=0, keepdims=True)
        tw_own[d] = jnp.where(sub == 0, t_row, jnp.where(sub == 1, w_row, 0.0))
    tw_own_local = pltpu.make_async_copy(tw_own.at[me], tw_ref.at[me], twr_sem.at[me])
    tw_own_local.start()

    def tw_send(off):
        d = lax.rem(me + off, n)
        return remote(tw_own.at[d], tw_ref.at[me], tws_sem.at[d], twr_sem.at[me], d)

    @pl.loop(1, n)
    def _(off):
        tw_send(off).start()

    own_x.wait()
    rope_cp.wait()
    x_send.wait_recv()

    def rope(t):
        return t * cs[0] + pltpu.roll(t, HEAD // 2, 1) * cs[1]

    def kv_send(h, side):
        dev = right if side == 0 else left
        return remote(kvb.at[chip, h], kvb.at[chip, h], kvs_sem.at[side, h], kvr_sem.at[side, h], dev)

    def kv_forward(h):
        even = h % 2 == 0
        src = lchip if even else rchip
        dev = right if even else left
        return remote(kvb.at[src, h], kvb.at[src, h], kvf_sem.at[h], kvr_sem.at[2, h], dev)

    @pl.loop(0, nk)
    def _(i):
        k_copy(0, 2 * i).wait()
        acc = jnp.dot(xf[...], wbuf[2 * i], preferred_element_type=F32)
        for hh in range(hpc):
            kvb[chip, hpc * i + hh, 0:ct] = rope(acc[:, hh * HEAD:(hh + 1) * HEAD]).astype(BF16)
        v_copy(0, 2 * i + 1).wait()
        acc = jnp.dot(xf[...], wbuf[2 * i + 1], preferred_element_type=F32)
        for hh in range(hpc):
            vt = acc[:, hh * HEAD:(hh + 1) * HEAD].T.astype(BF16)
            for b in range(ct // HEAD):
                kvb[chip, hpc * i + hh, ct + b * HEAD:ct + (b + 1) * HEAD] = vt[:, b * HEAD:(b + 1) * HEAD]
        for hh in range(hpc):
            for side in range(2):
                kv_send(hpc * i + hh, side).start()
        q_copy(nb - base_q + 2 * i, 2 * i).start()
        q_copy(nb - base_q + 2 * i + 1, 2 * i + 1).start()

    fwd_at = [nq * 5 // 12 + (nq * 2 // 12) * h for h in range(heads_c)]

    @pl.loop(0, nq)
    def _(i):
        slot = lax.rem(base_q + i, nb)
        q_copy(0, slot).wait()
        acc = jnp.dot(xf[...], wbuf[slot], preferred_element_type=F32)
        for hh in range(hpc):
            qt[hpc * i + hh] = rope(acc[:, hh * HEAD:(hh + 1) * HEAD]).T.astype(BF16)
        o_copy(i, slot).start()
        for h in range(heads_c):
            @pl.when(i == fwd_at[h])
            def _(h=h):
                kv_send(h, h % 2).wait_recv()
                kv_forward(h).start()

    ex = math.log2(math.e) / math.sqrt(HEAD)
    key_i = lax.broadcasted_iota(jnp.int32, (ct, ct), 0)
    qry_i = lax.broadcasted_iota(jnp.int32, (ct, ct), 1)

    def head(nc, h, g):
        q = qt[h * m + g]
        mx = None
        for j in range(nc):
            s = jnp.dot(kvb[j, h, 0:ct], q, preferred_element_type=F32)
            if j == nc - 1:
                s = jnp.where(key_i <= qry_i, s, -jnp.inf)
            st[j] = s
            sm = jnp.max(s, axis=0, keepdims=True)
            mx = sm if mx is None else jnp.maximum(mx, sm)
        tot = None
        for j in range(nc):
            p = jnp.exp2((st[j] - mx) * ex)
            st[j] = p
            ps = jnp.sum(p, axis=0, keepdims=True)
            tot = ps if tot is None else tot + ps
        inv = 1.0 / tot
        o = None
        for j in range(nc):
            vt = jnp.concatenate([kvb[j, h, ct + b * HEAD:ct + (b + 1) * HEAD] for b in range(ct // HEAD)], axis=1)
            oj = jnp.dot(vt, (st[j] * inv).astype(BF16), preferred_element_type=F32)
            o = oj if o is None else o + oj
        of[core * heads_c + h, :, ds(g * HEAD, HEAD)] = o.T.astype(BF16)

    def o_send(h):
        return remote(of.at[core * heads_c + h], of.at[core * heads_c + h], os_sem.at[h], or_sem.at[h], partner)

    @pl.loop(0, heads_c)
    def _(h):
        even = lax.rem(h, 2) == 0
        @pl.when(even)
        def _():
            kv_send(h, 1).wait_recv()

        @pl.when(jnp.logical_not(even))
        def _():
            kv_send(h, 0).wait_recv()

        remote(kvb.at[fchip, h], kvb.at[fchip, h], kvf_sem.at[h], kvr_sem.at[2, h], right).wait_recv()
        for nc in range(1, chips + 1):
            @pl.when(chip == nc - 1)
            def _(nc=nc):
                @pl.loop(0, m)
                def _(g):
                    head(nc, h, g)
        o_send(h).start()

    @pl.loop(0, heads_c)
    def _(h):
        pltpu.make_async_copy(of.at[(1 - core) * heads_c + h], of.at[(1 - core) * heads_c + h], or_sem.at[h]).wait()

    def place(c, j, who):
        return hg_ref.at[c * no + j, ds(who * ct, ct)]

    def h_local(j):
        return pltpu.make_async_copy(ho.at[j], place(core, j, chip), hl_sem.at[j])

    def h_send(j, side):
        dev = (right, left, partner)[side]
        return remote(ho.at[j], place(core, j, chip), hs_sem.at[side, j],
                      hr_sem.at[side, j] if side < 2 else pr_sem.at[0, j], dev)

    def h_forward(j, side):
        src = (lchip, rchip)[side]
        dev = (right, left)[side]
        return remote(place(core, j, src), place(core, j, src), hf_sem.at[j], hr_sem.at[2, j], dev)

    def h_pass(j, k):
        src = (None, lchip, rchip, fchip)[k]
        return remote(place(core, j, src), place(core, j, src), hp_sem.at[k - 1, j], pr_sem.at[k, j], partner)

    group = m * HEAD

    @pl.loop(0, no)
    def _(j):
        slot = lax.rem(base_q + nq + j, nb)
        o_copy(0, slot).wait()
        acc = None
        for g in range(kvh):
            t = jnp.dot(of[g], wbuf[slot, g * group:(g + 1) * group], preferred_element_type=F32)
            acc = t if acc is None else acc + t
        xs = xf[:, ds(core * (no * COL) + j * COL, COL)].astype(F32)
        ho[j] = (xs + acc).astype(BF16)
        h_send(j, 0).start()
        h_send(j, 1).start()
        h_send(j, 2).start()
        h_local(j).start()

    @pl.loop(0, no)
    def _(j):
        h_send(j, 0).wait_recv()
        even = lax.rem(j, 2) == 0

        @pl.when(even)
        def _():
            h_forward(j, 0).start()

        h_pass(j, 1).start()
        h_send(j, 1).wait_recv()

        @pl.when(jnp.logical_not(even))
        def _():
            h_forward(j, 1).start()

        h_pass(j, 2).start()

    @pl.loop(0, no)
    def _(j):
        h_forward(j, 0).wait_recv()
        h_pass(j, 3).start()

    @pl.loop(0, no)
    def _(j):
        for side in range(3):
            h_send(j, side).wait_send()
        h_local(j).wait()
        h_forward(j, 0).wait_send()
        for k in range(1, 4):
            h_pass(j, k).wait_send()
        for k in range(4):
            pltpu.make_async_copy(ho.at[j], place(core, j, chip), pr_sem.at[k, j]).wait()

    for h in range(heads_c):
        o_send(h).wait_send()
        kv_forward(h).wait_send()
        for side in range(2):
            kv_send(h, side).wait_send()
    x_send.wait_send()
    tw_own_local.wait()

    @pl.loop(1, n)
    def _(off):
        tw_send(off).wait_send()
        d = lax.rem(me + off, n)
        pltpu.make_async_copy(tw_own.at[d], tw_ref.at[d], twr_sem.at[d]).wait()


def build_kernel(n, me_ref, hg_ref, tw_ref, h_ref, buf_ref, pick, wcol):
    nch, toks, col = hg_ref.shape
    sd = h_ref.shape[0]
    per = buf_ref.shape[0]
    rows = tw_ref.shape[2]
    cap = rows // per

    @pl.when(pl.program_id(0) == 0)
    def _():
        li = lax.broadcasted_iota(jnp.int32, (rows, sd), 1).astype(F32)
        for s in range(n):
            t = jnp.broadcast_to(tw_ref[s, 0:1, :], (sd, rows)).T
            pick[s] = jnp.where(t == li, 1.0, 0.0).astype(BF16)
            wcol[s] = jnp.broadcast_to(tw_ref[s, 1:2, :], (sd, rows)).T

    for c in range(nch):
        h_ref[:, c * col:(c + 1) * col] = hg_ref[c, pl.ds(pl.multiple_of(me_ref[0] * sd, sd), sd), :]
        for s in range(n):
            r = jnp.dot(pick[s], hg_ref[c, s * sd:(s + 1) * sd, :], preferred_element_type=F32)
            w = jnp.concatenate([wcol[s]] * (col // sd), axis=1)
            r = (w * r).astype(BF16)
            for e in range(per):
                buf_ref[e, s * cap:(s + 1) * cap, c * col:(c + 1) * col] = r[e * cap:(e + 1) * cap]


def solution(mesh):
    n = mesh.shape["sp"]
    row = P(("dp", "sp"), None)
    full = P(None, None)

    def local(x, wq, wk, wv, wo, idx, probs):
        sd, hid = x.shape
        heads = wq.shape[1] // HEAD
        kvh = wk.shape[1] // HEAD
        m = heads // kvh
        ne = probs.shape[1]
        per = ne // n
        cap = 2 * sd * idx.shape[1] // ne
        rows = per * cap
        chips = n // CORES
        ct = CORES * sd
        hc = kvh // CORES
        no = hid // CORES // COL
        nq = hc * m * HEAD // COL
        nb = 12
        dma = pltpu.SemaphoreType.DMA
        any_ = pl.BlockSpec(memory_space=pl.ANY)
        vm = pl.BlockSpec(memory_space=pltpu.VMEM)
        hg, tw = pl.pallas_call(
            functools.partial(block_kernel, n, kvh, m, nb),
            out_shape=(jax.ShapeDtypeStruct((CORES * no, n * sd, COL), BF16),
                       jax.ShapeDtypeStruct((n, 8, rows), F32)),
            in_specs=[any_, any_, any_, any_, any_, vm, vm, any_],
            out_specs=(any_, any_),
            scratch_shapes=[
                pltpu.VMEM((ct, hid), BF16),
                pltpu.VMEM((nb, hid, COL), BF16),
                pltpu.VMEM((2, ct, HEAD), F32),
                pltpu.VMEM((chips, hc, 2 * ct, HEAD), BF16),
                pltpu.VMEM((hc * m, HEAD, ct), BF16),
                pltpu.VMEM((kvh, ct, m * HEAD), BF16),
                pltpu.VMEM((no, ct, COL), BF16),
                pltpu.VMEM((chips, ct, ct), F32),
                pltpu.VMEM((n, 8, rows), F32),
                dma((nb,)), dma((4,)), dma((n,)), dma((n,)),
                dma((2, hc)), dma((hc,)), dma((3, hc)), dma((hc,)), dma((hc,)),
                dma((no,)), dma((3, no)), dma((no,)), dma((3, no)), dma((3, no)), dma((4, no)),
            ],
            compiler_params=pltpu.CompilerParams(collective_id=0, has_side_effects=True,
                                                 vmem_limit_bytes=66_000_000),
        )(x, wq, wk, wv, wo, idx, probs, jnp.asarray(rope_table(n * sd)))

        step = 4
        me = lax.axis_index("sp").astype(jnp.int32).reshape(1)
        h, buf = pl.pallas_call(
            functools.partial(build_kernel, n),
            out_shape=(jax.ShapeDtypeStruct((sd, hid), BF16),
                       jax.ShapeDtypeStruct((per, n * cap, hid), BF16)),
            grid_spec=pltpu.PrefetchScalarGridSpec(
                num_scalar_prefetch=1, grid=(CORES * no // step,),
                in_specs=[pl.BlockSpec((step, n * sd, COL), lambda i, r: (i, 0, 0)),
                          pl.BlockSpec((n, 8, rows), lambda i, r: (0, 0, 0))],
                out_specs=(pl.BlockSpec((sd, step * COL), lambda i, r: (0, i)),
                           pl.BlockSpec((per, n * cap, step * COL), lambda i, r: (0, 0, i))),
                scratch_shapes=[pltpu.VMEM((n, rows, sd), BF16), pltpu.VMEM((n, rows, sd), F32)]),
        )(me, hg, tw)
        return h, buf

    return jax.shard_map(local, mesh=mesh, in_specs=(row, full, full, full, full, row, row), out_specs=(row, P(("dp", "sp"), None, None)), check_vma=False)
```

time: 335 us -> 135 us (0.40)
  blocking collectives: 143 us -> 0 us
  Pallas kernels: 0 us -> 131 us
  matrix products: 119 us -> 0 us
  waiting for transfers between devices: 27.9 us -> 0 us
  starting transfers between devices: 21.5 us -> 0 us
  local copies, waits for them, and re-layouts: 12.6 us -> 2.84 us
  other arithmetic: 9.62 us -> 0 us
    all_to_all x1 -> x0, blocking collectives: 143 us -> none  [local(): recv = lax.all_to_all(send, 'sp', 0, 0, tiled=True)]
    pallas_call x0 -> x2, Pallas kernels: none -> 131 us  [the longest x1 118 us: local(): pl.pallas_call(functools.partial(block_kernel, n, kvh, m, nb), out_shape=...]
    dot_general x16 -> x0, matrix products: 100 us -> none  [the longest x1 28.4 us: local(): jnp.dot(x, wq, preferred_element_type=jnp.float32).reshape(sd, heads, HEAD)]
    all_to_all x4 -> x0, waiting for transfers between devices: 27.9 us -> none  [the longest x1 19.9 us: local(): o = lax.all_to_all(o.reshape(s_len, g * m * HEAD), 'sp', 0, 1, tiled=True)]
    all_to_all x4 -> x0, starting transfers between devices: 21.5 us -> none  [the longest x1 6.14 us: local(): q = lax.all_to_all(q, 'sp', 1, 0, tiled=True)]
    sub x8 -> x0, matrix products: 18.8 us -> none  [block(): p = jax.nn.softmax(sc, axis=-1).astype(jnp.bfloat16)]
    le x8 -> x0, other arithmetic: 5.86 us -> none  [block(): keep = kpos[None, :] <= pj[:, None]]
    transpose x1 -> x0, local copies, waits for them, and re-layouts: 5.06 us -> none  [local(): recv.reshape(n, ne // n, cap, hid).transpose(1, 0, 2, 3)]
  transfers between devices with their start and end apart: 4 -> 0, of which waited for: 3 -> 0; matrix products, arithmetic and copies ran while one was open for 11% -> 0% of each run, Pallas kernels for 0% -> 0%
where the time goes in v1:
time: 135 us; the launch traced here: 134 us
  Pallas kernels  131 us (97%)
  local copies, waits for them, and re-layouts  2.84 us (2%)
    pallas_call x1, Pallas kernels, local(): pl.pallas_call(functools.partial(block_kernel, n, kvh, m, nb), out_shape=...  118 us
    pallas_call x1, Pallas kernels, local(): pl.pallas_call(functools.partial(build_kernel, n), out_shape=(jax.ShapeDt...  12.6 us
    unnamed x2, local copies, waits for them, and re-layouts  2.84 us

profile of v1, /device:TPU:113, one launch (start us, length us, event | category | flops | bytes accessed | tf_op | source)
XLA Modules:
  0.0 134.4 jit_solution(16514828022184494995)
XLA Ops:
  0.6 1.4 %copy.10.idx_ref = s32[128,4]{1,0:T(8,128)} copy(s32[128,4]{0,1:T(4,128)} %param.13) | data formatting | bytes 4096 | tf_op args[5]
  2.0 1.4 %copy.11.probs_ref = f32[128,16]{1,0:T(8,128)} copy(f32[128,16]{0,1:T(8,128)} %param.14) | data formatting | bytes 16384 | tf_op args[6]
  3.5 118.3 %shard_map.95 = (bf16[24,1024,256]{2,1,0:T(8,128)(2,1)}, f32[8,8,128]{2,1,0:T(8,128)}) custom-call(bf16[128,6144]{1,0:T(8,128)(2,1)} %x_ref.1, bf16[6144,6144]{1,0:T(8,128)(2,1)} %wq_ref.1, bf16[6144,1024]{1,0:T(8,128)(2,1)} %wk_ref.1, bf16[6144,1024]{1,0:T(8,128)(2,1)} %wv_ref.1, bf16[6144,6144]{1,0:T(8,128)(2,1)} %wo_ref.1, s32[128,4]{1,0:T(8,128)} %copy.10.idx_ref, ...), custom_call_target="tpu_custom_call" | custom-call | tf_op jit(solution)/shard_map/pallas_call | solution.py:376
  121.8 12.6 %shard_map.96 = (bf16[128,6144]{1,0:T(8,128)(2,1)}, bf16[2,512,6144]{2,1,0:T(8,128)(2,1)}) custom-call(s32[1]{0:T(128)} %bitcast.me_ref, bf16[24,1024,256]{2,1,0:T(8,128)(2,1)} %get-tuple-element.4.hg_ref, f32[8,8,128]{2,1,0:T(8,128)} %get-tuple-element.5.tw_ref), custom_call_target="tpu_custom_call" | custom-call | tf_op jit(solution)/shard_map/pallas_call | solution.py:402

commit v2 on v1

--- a/solution.py
+++ b/solution.py
@@ -26,7 +26,7 @@
 
 def block_kernel(n, kvh, m, nb, x_ref, wq_ref, wk_ref, wv_ref, wo_ref, idx_ref, probs_ref, rope_ref,
                  hg_ref, tw_ref,
-                 xf, wbuf, cs, kvb, qt, of, ho, st, tw_own,
+                 xf, wbuf, cs, kvb, qt, of, ho, st, accs, tw_own, idx_v, probs_v,
                  w_sem, x_sem, tws_sem, twr_sem, kvs_sem, kvf_sem, kvr_sem, os_sem, or_sem,
                  hl_sem, hs_sem, hf_sem, hp_sem, hr_sem, pr_sem):
     sd, hid = x_ref.shape
@@ -66,15 +66,17 @@
         return wcopy(wo_ref, core * (no * COL) + i * COL, slot)
 
     base_q = 2 * nk
-    for i in range(nk):
-        k_copy(i, 2 * i).start()
-        v_copy(i, 2 * i + 1).start()
     own_x = pltpu.make_async_copy(x_ref, xf.at[ds(core * sd, sd)], x_sem.at[2])
     own_x.start()
     rope_cp = pltpu.make_async_copy(rope_ref.at[:, ds(chip * ct, ct)], cs, x_sem.at[3])
     rope_cp.start()
-    for i in range(nb - base_q):
-        q_copy(i, base_q + i).start()
+    idx_cp = pltpu.make_async_copy(idx_ref, idx_v, x_sem.at[4])
+    idx_cp.start()
+    probs_cp = pltpu.make_async_copy(probs_ref, probs_v, x_sem.at[5])
+    probs_cp.start()
+    for i in range(nk):
+        k_copy(i, 2 * i).start()
+        v_copy(i, 2 * i + 1).start()
 
     barrier = pltpu.get_barrier_semaphore()
 
@@ -90,24 +92,28 @@
 
     x_send = remote(x_ref, xf.at[ds(core * sd, sd)], x_sem.at[0], x_sem.at[1], partner)
     x_send.start()
-
-    ne = probs_ref.shape[1]
-    top = idx_ref.shape[1]
+    for i in range(nb - base_q):
+        q_copy(i, base_q + i).start()
+
+    ne = probs_ref.shape[0]
+    top = idx_ref.shape[0]
     per = ne // n
     cap = 2 * sd * top // ne
-    probs = probs_ref[...]
-    ei = lax.broadcasted_iota(jnp.int32, (sd, ne), 1)
-    mine = jnp.zeros((sd, ne), F32)
-    tot = jnp.zeros((sd, 1), F32)
+    idx_cp.wait()
+    probs_cp.wait()
+    probs = probs_v[...]
+    ei = lax.broadcasted_iota(jnp.int32, (ne, sd), 0)
+    mine = jnp.zeros((ne, sd), F32)
+    tot = None
     for c in range(top):
-        hot = idx_ref[:, c:c + 1] == ei
+        hot = idx_v[c:c + 1, :] == ei
         mine = jnp.where(hot, 1.0, mine)
-        sel = jnp.sum(jnp.where(hot, probs, 0.0), axis=1, keepdims=True)
-        tot = sel if c == 0 else tot + sel
-    gate = probs / tot
-    low = (lax.broadcasted_iota(jnp.int32, (sd, sd), 1) < lax.broadcasted_iota(jnp.int32, (sd, sd), 0))
-    rank = jnp.dot(jnp.where(low, 1.0, 0.0).astype(BF16), mine.astype(BF16), preferred_element_type=F32)
-    rank = jnp.where(mine > 0.5, rank, -1.0)
+        sel = jnp.sum(jnp.where(hot, probs, 0.0), axis=0, keepdims=True)
+        tot = sel if tot is None else tot + sel
+    low = (lax.broadcasted_iota(jnp.int32, (sd, sd), 0) < lax.broadcasted_iota(jnp.int32, (sd, sd), 1))
+    rank = jnp.dot(mine.astype(BF16), jnp.where(low, 1.0, 0.0).astype(BF16), preferred_element_type=F32)
+    rank = jnp.where(mine > 0.5, rank, -1.0).T
+    gate = (probs / tot).T
     rows = per * cap
     lane = lax.broadcasted_iota(jnp.int32, (sd, rows), 1)
     tok1 = (lax.broadcasted_iota(jnp.int32, (sd, rows), 0) + 1).astype(F32)
@@ -153,13 +159,13 @@
     @pl.loop(0, nk)
     def _(i):
         k_copy(0, 2 * i).wait()
-        acc = jnp.dot(xf[...], wbuf[2 * i], preferred_element_type=F32)
+        v_copy(0, 2 * i + 1).wait()
+        ka = jnp.dot(xf[...], wbuf[2 * i], preferred_element_type=F32)
+        va = jnp.dot(xf[...], wbuf[2 * i + 1], preferred_element_type=F32)
         for hh in range(hpc):
-            kvb[chip, hpc * i + hh, 0:ct] = rope(acc[:, hh * HEAD:(hh + 1) * HEAD]).astype(BF16)
-        v_copy(0, 2 * i + 1).wait()
-        acc = jnp.dot(xf[...], wbuf[2 * i + 1], preferred_element_type=F32)
+            kvb[chip, hpc * i + hh, 0:ct] = rope(ka[:, hh * HEAD:(hh + 1) * HEAD]).astype(BF16)
         for hh in range(hpc):
-            vt = acc[:, hh * HEAD:(hh + 1) * HEAD].T.astype(BF16)
+            vt = va[:, hh * HEAD:(hh + 1) * HEAD].T.astype(BF16)
             for b in range(ct // HEAD):
                 kvb[chip, hpc * i + hh, ct + b * HEAD:ct + (b + 1) * HEAD] = vt[:, b * HEAD:(b + 1) * HEAD]
         for hh in range(hpc):
@@ -168,15 +174,19 @@
         q_copy(nb - base_q + 2 * i, 2 * i).start()
         q_copy(nb - base_q + 2 * i + 1, 2 * i + 1).start()
 
+    def q_store(i):
+        for hh in range(hpc):
+            qt[i, :, hh * ct:(hh + 1) * ct] = rope(accs[:, hh * HEAD:(hh + 1) * HEAD]).T.astype(BF16)
+
+    accs[...] = jnp.zeros_like(accs)
     fwd_at = [nq * 5 // 12 + (nq * 2 // 12) * h for h in range(heads_c)]
 
     @pl.loop(0, nq)
     def _(i):
         slot = lax.rem(base_q + i, nb)
         q_copy(0, slot).wait()
-        acc = jnp.dot(xf[...], wbuf[slot], preferred_element_type=F32)
-        for hh in range(hpc):
-            qt[hpc * i + hh] = rope(acc[:, hh * HEAD:(hh + 1) * HEAD]).T.astype(BF16)
+        q_store(jnp.maximum(i - 1, 0))
+        accs[...] = jnp.dot(xf[...], wbuf[slot], preferred_element_type=F32)
         o_copy(i, slot).start()
         for h in range(heads_c):
             @pl.when(i == fwd_at[h])
@@ -184,12 +194,14 @@
                 kv_send(h, h % 2).wait_recv()
                 kv_forward(h).start()
 
+    q_store(nq - 1)
     ex = math.log2(math.e) / math.sqrt(HEAD)
-    key_i = lax.broadcasted_iota(jnp.int32, (ct, ct), 0)
-    qry_i = lax.broadcasted_iota(jnp.int32, (ct, ct), 1)
-
-    def head(nc, h, g):
-        q = qt[h * m + g]
+    wide = hpc * ct
+    key_i = lax.broadcasted_iota(jnp.int32, (ct, wide), 0)
+    qry_i = lax.rem(lax.broadcasted_iota(jnp.int32, (ct, wide), 1), ct)
+
+    def attend(nc, h, g):
+        q = qt[h * (m // hpc) + g]
         mx = None
         for j in range(nc):
             s = jnp.dot(kvb[j, h, 0:ct], q, preferred_element_type=F32)
@@ -210,7 +222,8 @@
             vt = jnp.concatenate([kvb[j, h, ct + b * HEAD:ct + (b + 1) * HEAD] for b in range(ct // HEAD)], axis=1)
             oj = jnp.dot(vt, (st[j] * inv).astype(BF16), preferred_element_type=F32)
             o = oj if o is None else o + oj
-        of[core * heads_c + h, :, ds(g * HEAD, HEAD)] = o.T.astype(BF16)
+        o = jnp.concatenate([o[:, k * ct:(k + 1) * ct].T for k in range(hpc)], axis=1)
+        of[core * heads_c + h, :, ds(g * COL, COL)] = o.astype(BF16)
 
     def o_send(h):
         return remote(of.at[core * heads_c + h], of.at[core * heads_c + h], os_sem.at[h], or_sem.at[h], partner)
@@ -230,9 +243,9 @@
         for nc in range(1, chips + 1):
             @pl.when(chip == nc - 1)
             def _(nc=nc):
-                @pl.loop(0, m)
+                @pl.loop(0, m // hpc)
                 def _(g):
-                    head(nc, h, g)
+                    attend(nc, h, g)
         o_send(h).start()
 
     @pl.loop(0, heads_c)
@@ -372,30 +385,32 @@
         nb = 12
         dma = pltpu.SemaphoreType.DMA
         any_ = pl.BlockSpec(memory_space=pl.ANY)
-        vm = pl.BlockSpec(memory_space=pltpu.VMEM)
         hg, tw = pl.pallas_call(
             functools.partial(block_kernel, n, kvh, m, nb),
             out_shape=(jax.ShapeDtypeStruct((CORES * no, n * sd, COL), BF16),
                        jax.ShapeDtypeStruct((n, 8, rows), F32)),
-            in_specs=[any_, any_, any_, any_, any_, vm, vm, any_],
+            in_specs=[any_] * 8,
             out_specs=(any_, any_),
             scratch_shapes=[
                 pltpu.VMEM((ct, hid), BF16),
                 pltpu.VMEM((nb, hid, COL), BF16),
                 pltpu.VMEM((2, ct, HEAD), F32),
                 pltpu.VMEM((chips, hc, 2 * ct, HEAD), BF16),
-                pltpu.VMEM((hc * m, HEAD, ct), BF16),
+                pltpu.VMEM((nq, HEAD, COL // HEAD * ct), BF16),
                 pltpu.VMEM((kvh, ct, m * HEAD), BF16),
                 pltpu.VMEM((no, ct, COL), BF16),
-                pltpu.VMEM((chips, ct, ct), F32),
+                pltpu.VMEM((chips, ct, COL // HEAD * ct), F32),
+                pltpu.VMEM((ct, COL), F32),
                 pltpu.VMEM((n, 8, rows), F32),
-                dma((nb,)), dma((4,)), dma((n,)), dma((n,)),
+                pltpu.VMEM(idx.shape[::-1], jnp.int32),
+                pltpu.VMEM(probs.shape[::-1], F32),
+                dma((nb,)), dma((6,)), dma((n,)), dma((n,)),
                 dma((2, hc)), dma((hc,)), dma((3, hc)), dma((hc,)), dma((hc,)),
                 dma((no,)), dma((3, no)), dma((no,)), dma((3, no)), dma((3, no)), dma((4, no)),
             ],
             compiler_params=pltpu.CompilerParams(collective_id=0, has_side_effects=True,
                                                  vmem_limit_bytes=66_000_000),
-        )(x, wq, wk, wv, wo, idx, probs, jnp.asarray(rope_table(n * sd)))
+        )(x, wq, wk, wv, wo, idx.T, probs.T, jnp.asarray(rope_table(n * sd)))
 
         step = 4
         me = lax.axis_index("sp").astype(jnp.int32).reshape(1)

time: 135 us -> 112 us (0.83)
  Pallas kernels: 131 us -> 111 us
  local copies, waits for them, and re-layouts: 2.84 us -> 0 us
    pallas_call x1, Pallas kernels: 118 us -> 98.2 us  [local(): pl.pallas_call(functools.partial(block_kernel, n, kvh, m, nb), out_shape=...]
    unnamed x2 -> x0, local copies, waits for them, and re-layouts: 2.84 us -> none
where the time goes in v2:
time: 112 us; the launch traced here: 111 us
  Pallas kernels  111 us (99%)
    pallas_call x1, Pallas kernels, local(): pl.pallas_call(functools.partial(block_kernel, n, kvh, m, nb), out_shape=...  98.2 us
    pallas_call x1, Pallas kernels, local(): pl.pallas_call(functools.partial(build_kernel, n), out_shape=(jax.ShapeDt...  12.6 us

profile of v2, /device:TPU:113, one launch (start us, length us, event | category | flops | bytes accessed | tf_op | source)
XLA Modules:
  0.0 111.4 jit_solution(17544488761814706985)
XLA Ops:
  0.6 98.2 %shard_map.95 = (bf16[24,1024,256]{2,1,0:T(8,128)(2,1)}, f32[8,8,128]{2,1,0:T(8,128)}) custom-call(bf16[128,6144]{1,0:T(8,128)(2,1)} %x_ref.1, bf16[6144,6144]{1,0:T(8,128)(2,1)} %wq_ref.1, bf16[6144,1024]{1,0:T(8,128)(2,1)} %wk_ref.1, bf16[6144,1024]{1,0:T(8,128)(2,1)} %wv_ref.1, bf16[6144,6144]{1,0:T(8,128)(2,1)} %wo_ref.1, s32[4,128]{1,0:T(4,128)} %bitcast.4, ...), custom_call_target="tpu_custom_call" | custom-call | tf_op jit(solution)/shard_map/pallas_call | solution.py:388
  98.8 12.6 %shard_map.96 = (bf16[128,6144]{1,0:T(8,128)(2,1)}, bf16[2,512,6144]{2,1,0:T(8,128)(2,1)}) custom-call(s32[1]{0:T(128)} %bitcast.me_ref, bf16[24,1024,256]{2,1,0:T(8,128)(2,1)} %get-tuple-element.4.hg_ref, f32[8,8,128]{2,1,0:T(8,128)} %get-tuple-element.5.tw_ref), custom_call_target="tpu_custom_call" | custom-call | tf_op jit(solution)/shard_map/pallas_call | solution.py:417

commit v3 on v2

--- a/solution.py
+++ b/solution.py
@@ -25,8 +25,8 @@
 
 
 def block_kernel(n, kvh, m, nb, x_ref, wq_ref, wk_ref, wv_ref, wo_ref, idx_ref, probs_ref, rope_ref,
-                 hg_ref, tw_ref,
-                 xf, wbuf, cs, kvb, qt, of, ho, st, accs, tw_own, idx_v, probs_v,
+                 hg_ref, pick_ref, wcol_ref,
+                 xf, wbuf, cs, kvb, qt, of, ho, st, accs, tw_own, tw_all, idx_v, probs_v,
                  w_sem, x_sem, tws_sem, twr_sem, kvs_sem, kvf_sem, kvr_sem, os_sem, or_sem,
                  hl_sem, hs_sem, hf_sem, hp_sem, hr_sem, pr_sem):
     sd, hid = x_ref.shape
@@ -66,6 +66,18 @@
         return wcopy(wo_ref, core * (no * COL) + i * COL, slot)
 
     base_q = 2 * nk
+
+    def fetch(g):
+        slot = lax.rem(g, nb)
+
+        @pl.when(g < base_q + nq)
+        def _():
+            q_copy(g - base_q, slot).start()
+
+        @pl.when(jnp.logical_and(g >= base_q + nq, g < base_q + nq + no))
+        def _():
+            o_copy(g - base_q - nq, slot).start()
+
     own_x = pltpu.make_async_copy(x_ref, xf.at[ds(core * sd, sd)], x_sem.at[2])
     own_x.start()
     rope_cp = pltpu.make_async_copy(rope_ref.at[:, ds(chip * ct, ct)], cs, x_sem.at[3])
@@ -128,12 +140,12 @@
         t_row = jnp.sum(jnp.where(hit, tok1, 0.0), axis=0, keepdims=True) - 1.0
         w_row = jnp.sum(jnp.where(hit, gt, 0.0), axis=0, keepdims=True)
         tw_own[d] = jnp.where(sub == 0, t_row, jnp.where(sub == 1, w_row, 0.0))
-    tw_own_local = pltpu.make_async_copy(tw_own.at[me], tw_ref.at[me], twr_sem.at[me])
+    tw_own_local = pltpu.make_async_copy(tw_own.at[me], tw_all.at[me], twr_sem.at[me])
     tw_own_local.start()
 
     def tw_send(off):
         d = lax.rem(me + off, n)
-        return remote(tw_own.at[d], tw_ref.at[me], tws_sem.at[d], twr_sem.at[me], d)
+        return remote(tw_own.at[d], tw_all.at[me], tws_sem.at[d], twr_sem.at[me], d)
 
     @pl.loop(1, n)
     def _(off):
@@ -171,8 +183,8 @@
         for hh in range(hpc):
             for side in range(2):
                 kv_send(hpc * i + hh, side).start()
-        q_copy(nb - base_q + 2 * i, 2 * i).start()
-        q_copy(nb - base_q + 2 * i + 1, 2 * i + 1).start()
+        fetch(2 * i + nb)
+        fetch(2 * i + 1 + nb)
 
     def q_store(i):
         for hh in range(hpc):
@@ -187,7 +199,7 @@
         q_copy(0, slot).wait()
         q_store(jnp.maximum(i - 1, 0))
         accs[...] = jnp.dot(xf[...], wbuf[slot], preferred_element_type=F32)
-        o_copy(i, slot).start()
+        fetch(base_q + i + nb)
         for h in range(heads_c):
             @pl.when(i == fwd_at[h])
             def _(h=h):
@@ -200,30 +212,43 @@
     key_i = lax.broadcasted_iota(jnp.int32, (ct, wide), 0)
     qry_i = lax.rem(lax.broadcasted_iota(jnp.int32, (ct, wide), 1), ct)
 
-    def attend(nc, h, g):
-        q = qt[h * (m // hpc) + g]
-        mx = None
-        for j in range(nc):
-            s = jnp.dot(kvb[j, h, 0:ct], q, preferred_element_type=F32)
-            if j == nc - 1:
-                s = jnp.where(key_i <= qry_i, s, -jnp.inf)
-            st[j] = s
-            sm = jnp.max(s, axis=0, keepdims=True)
-            mx = sm if mx is None else jnp.maximum(mx, sm)
-        tot = None
-        for j in range(nc):
-            p = jnp.exp2((st[j] - mx) * ex)
-            st[j] = p
-            ps = jnp.sum(p, axis=0, keepdims=True)
-            tot = ps if tot is None else tot + ps
-        inv = 1.0 / tot
-        o = None
-        for j in range(nc):
-            vt = jnp.concatenate([kvb[j, h, ct + b * HEAD:ct + (b + 1) * HEAD] for b in range(ct // HEAD)], axis=1)
-            oj = jnp.dot(vt, (st[j] * inv).astype(BF16), preferred_element_type=F32)
-            o = oj if o is None else o + oj
-        o = jnp.concatenate([o[:, k * ct:(k + 1) * ct].T for k in range(hpc)], axis=1)
-        of[core * heads_c + h, :, ds(g * COL, COL)] = o.astype(BF16)
+    def attend(nc, h):
+        cnt = m // hpc
+        mx, inv = [None] * cnt, [None] * cnt
+
+        def scores(g):
+            q = qt[h * cnt + g]
+            for j in range(nc):
+                s = jnp.dot(kvb[j, h, 0:ct], q, preferred_element_type=F32)
+                if j == nc - 1:
+                    s = jnp.where(key_i <= qry_i, s, -jnp.inf)
+                st[g, j] = s
+                sm = jnp.max(s, axis=0, keepdims=True)
+                mx[g] = sm if j == 0 else jnp.maximum(mx[g], sm)
+
+        def soft(g):
+            for j in range(nc):
+                p = jnp.exp2((st[g, j] - mx[g]) * ex)
+                st[g, j] = p
+                ps = jnp.sum(p, axis=0, keepdims=True)
+                tot = ps if j == 0 else tot + ps
+            inv[g] = 1.0 / tot
+
+        def out(g):
+            for j in range(nc):
+                vt = jnp.concatenate([kvb[j, h, ct + b * HEAD:ct + (b + 1) * HEAD] for b in range(ct // HEAD)], axis=1)
+                oj = jnp.dot(vt, (st[g, j] * inv[g]).astype(BF16), preferred_element_type=F32)
+                o = oj if j == 0 else o + oj
+            o = jnp.concatenate([o[:, k * ct:(k + 1) * ct].T for k in range(hpc)], axis=1)
+            of[core * heads_c + h, :, g * COL:(g + 1) * COL] = o.astype(BF16)
+
+        for t in range(cnt + 2):
+            if t >= 2:
+                out(t - 2)
+            if t < cnt:
+                scores(t)
+            if 1 <= t < cnt + 1:
+                soft(t - 1)
 
     def o_send(h):
         return remote(of.at[core * heads_c + h], of.at[core * heads_c + h], os_sem.at[h], or_sem.at[h], partner)
@@ -243,9 +268,7 @@
         for nc in range(1, chips + 1):
             @pl.when(chip == nc - 1)
             def _(nc=nc):
-                @pl.loop(0, m // hpc)
-                def _(g):
-                    attend(nc, h, g)
+                attend(nc, h)
         o_send(h).start()
 
     @pl.loop(0, heads_c)
@@ -284,10 +307,26 @@
             acc = t if acc is None else acc + t
         xs = xf[:, ds(core * (no * COL) + j * COL, COL)].astype(F32)
         ho[j] = (xs + acc).astype(BF16)
+        fetch(base_q + nq + j + nb)
         h_send(j, 0).start()
         h_send(j, 1).start()
         h_send(j, 2).start()
         h_local(j).start()
+
+    tw_own_local.wait()
+
+    @pl.loop(1, n)
+    def _(off):
+        d = lax.rem(me + off, n)
+        pltpu.make_async_copy(tw_own.at[d], tw_all.at[d], twr_sem.at[d]).wait()
+
+    li = lax.broadcasted_iota(jnp.int32, (rows, sd), 1).astype(F32)
+
+    @pl.loop(0, n)
+    def _(s):
+        t = jnp.broadcast_to(tw_all[s, 0:1, :], (sd, rows)).T
+        pick_ref[s] = jnp.where(t == li, 1.0, 0.0).astype(BF16)
+        wcol_ref[s] = jnp.broadcast_to(tw_all[s, 1:2, :], (sd, rows)).T
 
     @pl.loop(0, no)
     def _(j):
@@ -329,38 +368,58 @@
         for side in range(2):
             kv_send(h, side).wait_send()
     x_send.wait_send()
-    tw_own_local.wait()
 
     @pl.loop(1, n)
     def _(off):
         tw_send(off).wait_send()
-        d = lax.rem(me + off, n)
-        pltpu.make_async_copy(tw_own.at[d], tw_ref.at[d], twr_sem.at[d]).wait()
-
-
-def build_kernel(n, me_ref, hg_ref, tw_ref, h_ref, buf_ref, pick, wcol):
+
+
+def build_kernel(n, step, hg_ref, pick, wcol, h_ref, buf_ref, stage, h_sem, b_sem):
     nch, toks, col = hg_ref.shape
-    sd = h_ref.shape[0]
+    sd = toks // n
     per = buf_ref.shape[0]
-    rows = tw_ref.shape[2]
+    rows = pick.shape[1]
     cap = rows // per
-
-    @pl.when(pl.program_id(0) == 0)
-    def _():
-        li = lax.broadcasted_iota(jnp.int32, (rows, sd), 1).astype(F32)
-        for s in range(n):
-            t = jnp.broadcast_to(tw_ref[s, 0:1, :], (sd, rows)).T
-            pick[s] = jnp.where(t == li, 1.0, 0.0).astype(BF16)
-            wcol[s] = jnp.broadcast_to(tw_ref[s, 1:2, :], (sd, rows)).T
-
-    for c in range(nch):
-        h_ref[:, c * col:(c + 1) * col] = hg_ref[c, pl.ds(pl.multiple_of(me_ref[0] * sd, sd), sd), :]
-        for s in range(n):
-            r = jnp.dot(pick[s], hg_ref[c, s * sd:(s + 1) * sd, :], preferred_element_type=F32)
-            w = jnp.concatenate([wcol[s]] * (col // sd), axis=1)
-            r = (w * r).astype(BF16)
-            for e in range(per):
-                buf_ref[e, s * cap:(s + 1) * cap, c * col:(c + 1) * col] = r[e * cap:(e + 1) * cap]
+    me = lax.axis_index("sp")
+
+    def ds(i, size):
+        return pl.ds(pl.multiple_of(i, size), size)
+
+    def h_copy(c):
+        return pltpu.make_async_copy(hg_ref.at[c, ds(me * sd, sd)], h_ref.at[:, ds(c * col, col)], h_sem.at[c])
+
+    def b_copy(i, slot):
+        return pltpu.make_async_copy(stage.at[slot], buf_ref.at[:, :, ds(i * (step * col), step * col)], b_sem.at[slot])
+
+    @pl.loop(0, nch)
+    def _(c):
+        h_copy(c).start()
+
+    slots = stage.shape[0]
+
+    @pl.loop(0, nch // step)
+    def _(i):
+        slot = lax.rem(i, slots)
+
+        @pl.when(i >= slots)
+        def _():
+            b_copy(i, slot).wait()
+
+        for k in range(step):
+            for s in range(n):
+                r = jnp.dot(pick[s], hg_ref[i * step + k, s * sd:(s + 1) * sd, :], preferred_element_type=F32)
+                w = jnp.concatenate([wcol[s]] * (col // sd), axis=1)
+                r = (w * r).astype(BF16)
+                for e in range(per):
+                    stage[slot, e, s * cap:(s + 1) * cap, k * col:(k + 1) * col] = r[e * cap:(e + 1) * cap]
+        b_copy(i, slot).start()
+
+    for k in range(slots):
+        b_copy(0, k).wait()
+
+    @pl.loop(0, nch)
+    def _(c):
+        h_copy(c).wait()
 
 
 def solution(mesh):
@@ -382,15 +441,17 @@
         hc = kvh // CORES
         no = hid // CORES // COL
         nq = hc * m * HEAD // COL
-        nb = 12
+        nb = 6
         dma = pltpu.SemaphoreType.DMA
         any_ = pl.BlockSpec(memory_space=pl.ANY)
-        hg, tw = pl.pallas_call(
+        vm = pl.BlockSpec(memory_space=pltpu.VMEM)
+        hg, pick, wcol = pl.pallas_call(
             functools.partial(block_kernel, n, kvh, m, nb),
-            out_shape=(jax.ShapeDtypeStruct((CORES * no, n * sd, COL), BF16),
-                       jax.ShapeDtypeStruct((n, 8, rows), F32)),
+            out_shape=(pltpu.VMEM((CORES * no, n * sd, COL), BF16),
+                       pltpu.VMEM((n, rows, sd), BF16),
+                       pltpu.VMEM((n, rows, sd), F32)),
             in_specs=[any_] * 8,
-            out_specs=(any_, any_),
+            out_specs=(any_, vm, vm),
             scratch_shapes=[
                 pltpu.VMEM((ct, hid), BF16),
                 pltpu.VMEM((nb, hid, COL), BF16),
@@ -399,8 +460,9 @@
                 pltpu.VMEM((nq, HEAD, COL // HEAD * ct), BF16),
                 pltpu.VMEM((kvh, ct, m * HEAD), BF16),
                 pltpu.VMEM((no, ct, COL), BF16),
-                pltpu.VMEM((chips, ct, COL // HEAD * ct), F32),
+                pltpu.VMEM((m * HEAD // COL, chips, ct, COL // HEAD * ct), F32),
                 pltpu.VMEM((ct, COL), F32),
+                pltpu.VMEM((n, 8, rows), F32),
                 pltpu.VMEM((n, 8, rows), F32),
                 pltpu.VMEM(idx.shape[::-1], jnp.int32),
                 pltpu.VMEM(probs.shape[::-1], F32),
@@ -409,23 +471,21 @@
                 dma((no,)), dma((3, no)), dma((no,)), dma((3, no)), dma((3, no)), dma((4, no)),
             ],
             compiler_params=pltpu.CompilerParams(collective_id=0, has_side_effects=True,
-                                                 vmem_limit_bytes=66_000_000),
-        )(x, wq, wk, wv, wo, idx.T, probs.T, jnp.asarray(rope_table(n * sd)))
-
-        step = 4
-        me = lax.axis_index("sp").astype(jnp.int32).reshape(1)
+                                                 vmem_limit_bytes=50_000_000),
+        )(*(pltpu.with_memory_space_constraint(a, pltpu.HBM)
+            for a in (x, wq, wk, wv, wo, idx.T, probs.T, jnp.asarray(rope_table(n * sd)))))
+
+        step = 2
         h, buf = pl.pallas_call(
-            functools.partial(build_kernel, n),
+            functools.partial(build_kernel, n, step),
             out_shape=(jax.ShapeDtypeStruct((sd, hid), BF16),
                        jax.ShapeDtypeStruct((per, n * cap, hid), BF16)),
-            grid_spec=pltpu.PrefetchScalarGridSpec(
-                num_scalar_prefetch=1, grid=(CORES * no // step,),
-                in_specs=[pl.BlockSpec((step, n * sd, COL), lambda i, r: (i, 0, 0)),
-                          pl.BlockSpec((n, 8, rows), lambda i, r: (0, 0, 0))],
-                out_specs=(pl.BlockSpec((sd, step * COL), lambda i, r: (0, i)),
-                           pl.BlockSpec((per, n * cap, step * COL), lambda i, r: (0, 0, i))),
-                scratch_shapes=[pltpu.VMEM((n, rows, sd), BF16), pltpu.VMEM((n, rows, sd), F32)]),
-        )(me, hg, tw)
+            in_specs=[vm, vm, vm],
+            out_specs=(any_, any_),
+            scratch_shapes=[pltpu.VMEM((3, per, n * cap, step * COL), BF16),
+                            dma((CORES * no,)), dma((3,))],
+            compiler_params=pltpu.CompilerParams(vmem_limit_bytes=30_000_000),
+        )(hg, pick, wcol)
         return h, buf
 
     return jax.shard_map(local, mesh=mesh, in_specs=(row, full, full, full, full, row, row), out_specs=(row, P(("dp", "sp"), None, None)), check_vma=False)

time: 112 us -> 103 us (0.920)
  Pallas kernels: 111 us -> 102 us
    pallas_call x1, Pallas kernels: 12.6 us -> 7.03 us  [local(): pl.pallas_call(functools.partial(build_kernel, n, step), out_shape=(jax.S...]
    pallas_call x1, Pallas kernels: 98.2 us -> 95.2 us  [local(): pl.pallas_call(functools.partial(block_kernel, n, kvh, m, nb), out_shape=...]
where the time goes in v3:
time: 103 us
  Pallas kernels  102 us (99%)
    pallas_call x1, Pallas kernels, local(): pl.pallas_call(functools.partial(block_kernel, n, kvh, m, nb), out_shape=...  95.2 us
    pallas_call x1, Pallas kernels, local(): pl.pallas_call(functools.partial(build_kernel, n, step), out_shape=(jax.S...  7.03 us

profile of v3, /device:TPU:113, one launch (start us, length us, event | category | flops | bytes accessed | tf_op | source)
XLA Modules:
  0.0 102.8 jit_solution(18113005937154771792)
XLA Ops:
  0.6 95.2 %shard_map.95 = (bf16[24,1024,256]{2,1,0:T(8,128)(2,1)S(1)}, bf16[8,128,128]{2,1,0:T(8,128)(2,1)S(1)}, f32[8,128,128]{2,1,0:T(8,128)S(1)}) custom-call(bf16[128,6144]{1,0:T(8,128)(2,1)} %x_ref.1, bf16[6144,6144]{1,0:T(8,128)(2,1)} %wq_ref.1, bf16[6144,1024]{1,0:T(8,128)(2,1)} %wk_ref.1, bf16[6144,1024]{1,0:T(8,128)(2,1)} %wv_ref.1, ...), custom_call_target="tpu_custom_call" | custom-call | tf_op jit(solution)/shard_map/pallas_call | solution.py:448
  95.8 7.0 %shard_map.96 = (bf16[128,6144]{1,0:T(8,128)(2,1)}, bf16[2,512,6144]{2,1,0:T(8,128)(2,1)}) custom-call(bf16[24,1024,256]{2,1,0:T(8,128)(2,1)S(1)} %get-tuple-element.5.hg_ref, bf16[8,128,128]{2,1,0:T(8,128)(2,1)S(1)} %get-tuple-element.6.pick, f32[8,128,128]{2,1,0:T(8,128)S(1)} %get-tuple-element.7.wcol), custom_call_target="tpu_custom_call" | custom-call | tf_op jit(solution)/shard_map/pallas_call | solution.py:479

commit v4 on v3

--- a/solution.py
+++ b/solution.py
@@ -11,6 +11,7 @@
 HEAD = 128
 ROPE_BASE = 1000000.0
 CORES = 2
+SHIFT = 1
 COL = 256
 F32 = jnp.float32
 BF16 = jnp.bfloat16
@@ -289,13 +290,22 @@
     def h_forward(j, side):
         src = (lchip, rchip)[side]
         dev = (right, left)[side]
-        return remote(place(core, j, src), place(core, j, src), hf_sem.at[j], hr_sem.at[2, j], dev)
+        return remote(place(core, j, src), place(core, j, src), hf_sem.at[side, j], hr_sem.at[2, j], dev)
 
     def h_pass(j, k):
         src = (None, lchip, rchip, fchip)[k]
         return remote(place(core, j, src), place(core, j, src), hp_sem.at[k - 1, j], pr_sem.at[k, j], partner)
 
     group = m * HEAD
+
+    last = chip == chips - 1
+    across = chip == lax.rem(chips + 1, chips)
+
+    def sends_on(j, side):
+        kind = lax.rem(j, 2) == side
+        late = j >= no - 2 * SHIFT
+        return jnp.logical_or(jnp.logical_and(kind, jnp.logical_not(jnp.logical_and(late, last))),
+                              jnp.logical_and(late, across))
 
     @pl.loop(0, no)
     def _(j):
@@ -331,16 +341,15 @@
     @pl.loop(0, no)
     def _(j):
         h_send(j, 0).wait_recv()
-        even = lax.rem(j, 2) == 0
-
-        @pl.when(even)
+
+        @pl.when(sends_on(j, 0))
         def _():
             h_forward(j, 0).start()
 
         h_pass(j, 1).start()
         h_send(j, 1).wait_recv()
 
-        @pl.when(jnp.logical_not(even))
+        @pl.when(sends_on(j, 1))
         def _():
             h_forward(j, 1).start()
 
@@ -356,7 +365,10 @@
         for side in range(3):
             h_send(j, side).wait_send()
         h_local(j).wait()
-        h_forward(j, 0).wait_send()
+        for side in range(2):
+            @pl.when(sends_on(j, side))
+            def _(side=side):
+                h_forward(j, side).wait_send()
         for k in range(1, 4):
             h_pass(j, k).wait_send()
         for k in range(4):
@@ -468,7 +480,7 @@
                 pltpu.VMEM(probs.shape[::-1], F32),
                 dma((nb,)), dma((6,)), dma((n,)), dma((n,)),
                 dma((2, hc)), dma((hc,)), dma((3, hc)), dma((hc,)), dma((hc,)),
-                dma((no,)), dma((3, no)), dma((no,)), dma((3, no)), dma((3, no)), dma((4, no)),
+                dma((no,)), dma((3, no)), dma((2, no)), dma((3, no)), dma((3, no)), dma((4, no)),
             ],
             compiler_params=pltpu.CompilerParams(collective_id=0, has_side_effects=True,
                                                  vmem_limit_bytes=50_000_000),

time: 103 us -> 101 us (0.981)
  Pallas kernels: 102 us -> 100 us
    pallas_call x1, Pallas kernels: 95.2 us -> 93.2 us  [local(): pl.pallas_call(functools.partial(block_kernel, n, kvh, m, nb), out_shape=...]
where the time goes in v4:
time: 101 us
  Pallas kernels  100 us (99%)
    pallas_call x1, Pallas kernels, local(): pl.pallas_call(functools.partial(block_kernel, n, kvh, m, nb), out_shape=...  93.2 us
    pallas_call x1, Pallas kernels, local(): pl.pallas_call(functools.partial(build_kernel, n, step), out_shape=(jax.S...  7.03 us

profile of v4, /device:TPU:113, one launch (start us, length us, event | category | flops | bytes accessed | tf_op | source)
XLA Modules:
  0.0 100.9 jit_solution(4482487028355084063)
XLA Ops:
  0.6 93.2 %shard_map.95 = (bf16[24,1024,256]{2,1,0:T(8,128)(2,1)S(1)}, bf16[8,128,128]{2,1,0:T(8,128)(2,1)S(1)}, f32[8,128,128]{2,1,0:T(8,128)S(1)}) custom-call(bf16[128,6144]{1,0:T(8,128)(2,1)} %x_ref.1, bf16[6144,6144]{1,0:T(8,128)(2,1)} %wq_ref.1, bf16[6144,1024]{1,0:T(8,128)(2,1)} %wk_ref.1, bf16[6144,1024]{1,0:T(8,128)(2,1)} %wv_ref.1, ...), custom_call_target="tpu_custom_call" | custom-call | tf_op jit(solution)/shard_map/pallas_call | solution.py:460
  93.9 7.0 %shard_map.96 = (bf16[128,6144]{1,0:T(8,128)(2,1)}, bf16[2,512,6144]{2,1,0:T(8,128)(2,1)}) custom-call(bf16[24,1024,256]{2,1,0:T(8,128)(2,1)S(1)} %get-tuple-element.5.hg_ref, bf16[8,128,128]{2,1,0:T(8,128)(2,1)S(1)} %get-tuple-element.6.pick, f32[8,128,128]{2,1,0:T(8,128)S(1)} %get-tuple-element.7.wcol), custom_call_target="tpu_custom_call" | custom-call | tf_op jit(solution)/shard_map/pallas_call | solution.py:491

commit v5 on v4

--- a/solution.py
+++ b/solution.py
@@ -487,7 +487,7 @@
         )(*(pltpu.with_memory_space_constraint(a, pltpu.HBM)
             for a in (x, wq, wk, wv, wo, idx.T, probs.T, jnp.asarray(rope_table(n * sd)))))
 
-        step = 2
+        step = 3
         h, buf = pl.pallas_call(
             functools.partial(build_kernel, n, step),
             out_shape=(jax.ShapeDtypeStruct((sd, hid), BF16),

time: 101 us -> 100 us (0.990)
  no operation moved by 1% of the time
where the time goes in v5:
time: 100 us
  Pallas kernels  99.5 us (100%)
    pallas_call x1, Pallas kernels, local(): pl.pallas_call(functools.partial(block_kernel, n, kvh, m, nb), out_shape=...  93.2 us
    pallas_call x1, Pallas kernels, local(): pl.pallas_call(functools.partial(build_kernel, n, step), out_shape=(jax.S...  6.28 us

profile of v5, /device:TPU:113, one launch (start us, length us, event | category | flops | bytes accessed | tf_op | source)
XLA Modules:
  0.0 100.1 jit_solution(128092157185845765)
XLA Ops:
  0.6 93.2 %shard_map.95 = (bf16[24,1024,256]{2,1,0:T(8,128)(2,1)S(1)}, bf16[8,128,128]{2,1,0:T(8,128)(2,1)S(1)}, f32[8,128,128]{2,1,0:T(8,128)S(1)}) custom-call(bf16[128,6144]{1,0:T(8,128)(2,1)} %x_ref.1, bf16[6144,6144]{1,0:T(8,128)(2,1)} %wq_ref.1, bf16[6144,1024]{1,0:T(8,128)(2,1)} %wk_ref.1, bf16[6144,1024]{1,0:T(8,128)(2,1)} %wv_ref.1, ...), custom_call_target="tpu_custom_call" | custom-call | tf_op jit(solution)/shard_map/pallas_call | solution.py:460
  93.9 6.3 %shard_map.96 = (bf16[128,6144]{1,0:T(8,128)(2,1)}, bf16[2,512,6144]{2,1,0:T(8,128)(2,1)}) custom-call(bf16[24,1024,256]{2,1,0:T(8,128)(2,1)S(1)} %get-tuple-element.5.hg_ref, bf16[8,128,128]{2,1,0:T(8,128)(2,1)S(1)} %get-tuple-element.6.pick, f32[8,128,128]{2,1,0:T(8,128)S(1)} %get-tuple-element.7.wcol), custom_call_target="tpu_custom_call" | custom-call | tf_op jit(solution)/shard_map/pallas_call | solution.py:491

commit v6 on v5

--- a/solution.py
+++ b/solution.py
@@ -494,8 +494,8 @@
                        jax.ShapeDtypeStruct((per, n * cap, hid), BF16)),
             in_specs=[vm, vm, vm],
             out_specs=(any_, any_),
-            scratch_shapes=[pltpu.VMEM((3, per, n * cap, step * COL), BF16),
-                            dma((CORES * no,)), dma((3,))],
+            scratch_shapes=[pltpu.VMEM((4, per, n * cap, step * COL), BF16),
+                            dma((CORES * no,)), dma((4,))],
             compiler_params=pltpu.CompilerParams(vmem_limit_bytes=30_000_000),
         )(hg, pick, wcol)
         return h, buf

time: 100 us -> 100 us (level)
  no operation moved by 1% of the time
where the time goes in v6:
time: 100 us
  Pallas kernels  99.5 us (100%)
    pallas_call x1, Pallas kernels, local(): pl.pallas_call(functools.partial(block_kernel, n, kvh, m, nb), out_shape=...  93.2 us
    pallas_call x1, Pallas kernels, local(): pl.pallas_call(functools.partial(build_kernel, n, step), out_shape=(jax.S...  6.26 us

profile of v6, /device:TPU:113, one launch (start us, length us, event | category | flops | bytes accessed | tf_op | source)
XLA Modules:
  0.0 100.1 jit_solution(3266292461283239540)
XLA Ops:
  0.6 93.2 %shard_map.95 = (bf16[24,1024,256]{2,1,0:T(8,128)(2,1)S(1)}, bf16[8,128,128]{2,1,0:T(8,128)(2,1)S(1)}, f32[8,128,128]{2,1,0:T(8,128)S(1)}) custom-call(bf16[128,6144]{1,0:T(8,128)(2,1)} %x_ref.1, bf16[6144,6144]{1,0:T(8,128)(2,1)} %wq_ref.1, bf16[6144,1024]{1,0:T(8,128)(2,1)} %wk_ref.1, bf16[6144,1024]{1,0:T(8,128)(2,1)} %wv_ref.1, ...), custom_call_target="tpu_custom_call" | custom-call | tf_op jit(solution)/shard_map/pallas_call | solution.py:460
  93.9 6.3 %shard_map.96 = (bf16[128,6144]{1,0:T(8,128)(2,1)}, bf16[2,512,6144]{2,1,0:T(8,128)(2,1)}) custom-call(bf16[24,1024,256]{2,1,0:T(8,128)(2,1)S(1)} %get-tuple-element.5.hg_ref, bf16[8,128,128]{2,1,0:T(8,128)(2,1)S(1)} %get-tuple-element.6.pick, f32[8,128,128]{2,1,0:T(8,128)S(1)} %get-tuple-element.7.wcol), custom_call_target="tpu_custom_call" | custom-call | tf_op jit(solution)/shard_map/pallas_call | solution.py:491
